TPU v7x, 128 devices: a whole 4x4x4 slice. The times are simulated.
128 devices in a mesh: m: 1, kk: 16 (over z, y), g: 8 (over x, core).
Axes of the slice: x: 4, y: 4, z: 4, core: 2. Of those that a mesh axis runs over, the one named last changes fastest.
Arguments:
- a_mat: bfloat16 [8192, 8192], P(('m', 'g'), 'kk')
Outputs:
- output: float32 [8, 5, 1024, 1024], P(('m', 'g'), None, 'kk')
All inputs are finite; a program needn't handle non-finite values.
Results may differ from a plain program's by a relative error of at most 0.001.
Values are sent between devices in bfloat16 or wider.
A program may use at most 1 GiB of HBM per device.

v0:
```python
import math
import jax
import jax.numpy as jnp
from jax import lax
from jax.sharding import PartitionSpec as P


def block_offsets(groups):
    half_size = groups // 2
    step_width = max(1, math.isqrt(half_size))
    big_count = -(-half_size // step_width)
    small_offs = [step_width - 1 - pos_idx for pos_idx in range(step_width)]
    big_offs = [(pos_idx + 1) * step_width for pos_idx in range(big_count)]
    return half_size, small_offs, big_offs


def solution(mesh):
    groups = mesh.shape["g"]
    half_size, small_offs, big_offs = block_offsets(groups)
    has_empty = 2 * half_size == groups

    def fetch_block(a_blk, offset):
        if offset == 0:
            return a_blk
        perm_pairs = [((dest_pos + offset) % groups, dest_pos) for dest_pos in range(groups)]
        return lax.ppermute(a_blk, "g", perm_pairs)

    def local_fn(a_blk):
        dev_pos = lax.axis_index("g")
        rows_blk = a_blk.shape[0]
        small_stack = jnp.stack([fetch_block(a_blk, offset) for offset in small_offs])
        big_stack = jnp.stack([fetch_block(a_blk, offset) for offset in big_offs])
        diag_blk = lax.dot_general(a_blk, a_blk, (((1,), (1,)), ((), ())), preferred_element_type=jnp.float32)
        cross_blk = jnp.einsum("jrk,isk->jirs", big_stack, small_stack, preferred_element_type=jnp.float32)
        cross_blk = cross_blk.reshape(-1, rows_blk, rows_blk)[:half_size]
        result = jnp.concatenate([diag_blk[None], cross_blk], axis=0)
        if has_empty:
            slot_ids = jnp.arange(half_size + 1)[:, None, None]
            result = jnp.where((slot_ids == half_size) & (dev_pos >= half_size), 0.0, result)
        result = lax.psum_scatter(result, "kk", scatter_dimension=1, tiled=True)
        return result[None]

    return jax.shard_map(local_fn, mesh=mesh, in_specs=(P(("m", "g"), "kk"),), out_specs=P(("m", "g"), None, "kk", None), check_vma=False)
```

profile of v0, /device:TPU:1, one launch (start us, length us, event | category | flops | bytes accessed | tf_op | source)
XLA Modules:
  0.0 250.1 jit_solution(17576175242095539648)
XLA Ops:
  6.5 0.0 reduce-scatter.2.cloned.1.call-start
  6.5 1.4 collective-permute-start
  7.9 2.9 %collective-permute-start.2 = (bf16[1024,512]{1,0:T(8,128)(2,1)}, bf16[1024,512]{1,0:T(8,128)(2,1)S(1)}, u32[]{:S(2)}, u32[]{:S(2)}) collective-permute-start(bf16[1024,512]{1,0:T(8,128)(2,1)} %param.1), channel_id=1, source_target_pairs={{4,0},{5,1},{6,2},{7,3},{0,4},{1,5},{2,6},{3,7},{12,8},{13,9},{14,... | collective-permute-start | bytes 3145736 | tf_op jit(solution)/shard_map/ppermute | solution.py:26
  10.8 0.9 collective-permute-start.1
  11.7 0.0 copy-start
  11.7 4.9 %convolution_bitcast_fusion.1 = f32[1,1024,1024]{2,1,0:T(8,128)} fusion(bf16[1024,512]{1,0:T(8,128)(2,1)} %param.1), kind=kOutput, calls=%fused_computation.2 | convolution fusion | flops 1073741824 | bytes 5242880 | tf_op jit(solution)/shard_map/dot_general | solution.py:33
  16.5 15.0 %collective-permute-done = bf16[1024,512]{1,0:T(8,128)(2,1)S(1)} collective-permute-done((bf16[1024,512]{1,0:T(8,128)(2,1)}, bf16[1024,512]{1,0:T(8,128)(2,1)S(1)}, u32[]{:S(2)}, u32[]{:S(2)}) %collective-permute-start) | collective-permute-done | bytes 1048608 | tf_op jit(solution)/shard_map/ppermute | solution.py:26
  31.5 1.8 collective-permute-done.2
  33.3 24.0 %collective-permute-done.1 = bf16[1024,512]{1,0:T(8,128)(2,1)S(1)} collective-permute-done((bf16[1024,512]{1,0:T(8,128)(2,1)}, bf16[1024,512]{1,0:T(8,128)(2,1)S(1)}, u32[]{:S(2)}, u32[]{:S(2)}) %collective-permute-start.1) | collective-permute-done | bytes 1048608 | tf_op jit(solution)/shard_map/ppermute | solution.py:26
  57.3 0.0 copy-done
  57.3 8.3 %convolution_bitcast_fusion = f32[2,2,1024,1024]{2,3,0,1:T(8,128)} fusion(bf16[1,1024,512]{2,1,0:T(8,128)(2,1)S(1)} %bitcast.21, bf16[1,1024,512]{2,1,0:T(8,128)(2,1)S(1)} %bitcast.22, bf16[1,1024,512]{2,1,0:T(8,128)(2,1)S(1)} %bitcast.23, bf16[1,1024,512]{2,1,0:T(8,128)(2,1)S(1)} %bitcast.24), kind=kOutput, calls=%fused_computation.1 | convolution fusion | flops 4303355904 | bytes 20971520 | tf_op jit(solution)/shard_map/jrk,isk->jirs/dot_general | solution.py:34
  65.6 16.4 %copy.2 = f32[2,2,1024,1024]{3,2,1,0:T(8,128)} copy(f32[2,2,1024,1024]{2,3,0,1:T(8,128)} %convolution_bitcast_fusion) | data formatting | bytes 33554432 | tf_op jit(solution)/shard_map/jrk,isk->jirs/transpose | solution.py:34
  82.0 16.9 %maximum_select_fusion = f32[5,1024,1024]{2,1,0:T(8,128)} fusion(f32[4,1024,1024]{2,1,0:T(8,128)} %bitcast.20, f32[1,1024,1024]{2,1,0:T(8,128)} %convolution_bitcast_fusion.1, pred[5]{0:T(512)(128)(4,1)S(1)} %compare_and_fusion), kind=kLoop, calls=%fused_computation | loop fusion | flops 10485760 | bytes 41943044 | tf_op jit(solution)/shard_map/jit(_where)/select_n | solution.py:39
  98.9 0.0 reduce-scatter.2.cloned.1.call-update
  98.9 144.4 %reduce-scatter.2.cloned.1.call-done = f32[5,64,1024]{2,1,0:T(8,128)} async-done(((f32[5,1024,1024]{2,1,0:T(8,128)}), f32[5,64,1024]{2,1,0:T(8,128)}) %reduce-scatter.2.cloned.1.call-update) | async-done | bytes 1310736 | tf_op jit(solution)/shard_map/reduce_scatter | solution.py:40
  (1 shorter events, 0.0 us)
Async XLA Ops:
  6.5 236.7 %reduce-scatter.2.cloned.1.call-start = ((), (), s32[]{:S(2)}) async-start(), calls=%async_computation.1 | async-start | bytes 22282240 | tf_op jit(solution)/shard_map/reduce_scatter | solution.py:40
  6.5 24.9 %collective-permute-start = (bf16[1024,512]{1,0:T(8,128)(2,1)}, bf16[1024,512]{1,0:T(8,128)(2,1)S(1)}, u32[]{:S(2)}, u32[]{:S(2)}) collective-permute-start(bf16[1024,512]{1,0:T(8,128)(2,1)} %param.1), channel_id=1, source_target_pairs={{1,0},{2,1},{3,2},{4,3},{5,4},{6,5},{7,6},{0,7},{9,8},{10,9},{11,1... | collective-permute-start | bytes 3145736 | tf_op jit(solution)/shard_map/ppermute | solution.py:26
  7.9 25.4 %collective-permute-start.2 = (bf16[1024,512]{1,0:T(8,128)(2,1)}, bf16[1024,512]{1,0:T(8,128)(2,1)S(1)}, u32[]{:S(2)}, u32[]{:S(2)}) collective-permute-start(bf16[1024,512]{1,0:T(8,128)(2,1)} %param.1), channel_id=1, source_target_pairs={{4,0},{5,1},{6,2},{7,3},{0,4},{1,5},{2,6},{3,7},{12,8},{13,9},{14,... | collective-permute-start | bytes 3145736 | tf_op jit(solution)/shard_map/ppermute | solution.py:26
  10.8 46.5 %collective-permute-start.1 = (bf16[1024,512]{1,0:T(8,128)(2,1)}, bf16[1024,512]{1,0:T(8,128)(2,1)S(1)}, u32[]{:S(2)}, u32[]{:S(2)}) collective-permute-start(bf16[1024,512]{1,0:T(8,128)(2,1)} %param.1), channel_id=1, source_target_pairs={{2,0},{3,1},{4,2},{5,3},{6,4},{7,5},{0,6},{1,7},{10,8},{11,9},{12,... | collective-permute-start | bytes 3145736 | tf_op jit(solution)/shard_map/ppermute | solution.py:26
  11.7 45.6 %copy-start = (bf16[1024,512]{1,0:T(8,128)(2,1)S(1)}, bf16[1024,512]{1,0:T(8,128)(2,1)}, u32[]{:S(2)}) copy-start(bf16[1024,512]{1,0:T(8,128)(2,1)} %param.1) | copy-start | bytes 3145732
Sparse Core Ops, SparseCore 0:
  99.0 144.2 reduce-scatter.1
where the time goes:
time: 251 us; the launch traced here: 250 us
  waiting for transfers between devices  185 us (74%)
  other arithmetic  16.9 us (7%)
  local copies, waits for them, and re-layouts  16.4 us (7%)
  between operations  13.4 us (5%)
  matrix products  13.1 us (5%)
  starting transfers between devices  5.11 us (2%)
    reduce_scatter x1, waiting for transfers between devices, local_fn(): result = lax.psum_scatter(result, 'kk', scatter_dimension=1, tiled=True)  144 us
    ppermute x3, waiting for transfers between devices, fetch_block(): return lax.ppermute(a_blk, 'g', perm_pairs)  40.8 us
    select_n x1, other arithmetic, local_fn(): jnp.where((slot_ids == half_size) & (dev_pos >= half_size), 0.0, result)  16.9 us
    transpose x1, local copies, waits for them, and re-layouts, local_fn(): jnp.einsum('jrk,isk->jirs', big_stack, small_stack, preferred_element_typ...  16.4 us
    dot_general x1, matrix products, local_fn(): jnp.einsum('jrk,isk->jirs', big_stack, small_stack, preferred_element_typ...  8.26 us
    ppermute x3, starting transfers between devices, fetch_block(): return lax.ppermute(a_blk, 'g', perm_pairs)  5.11 us
  transfers between devices with their start and end apart: 4, of which 4 were waited for; matrix products, arithmetic and copies ran while one was open for 2% of the time, Pallas kernels for 0%

commit v1 on v0

v1 whole, which is shorter than its diff:
```python
import functools
import jax
import jax.numpy as jnp
from jax import lax
from jax.experimental import pallas as pl
from jax.experimental.pallas import tpu as pltpu
from jax.sharding import PartitionSpec as P

MESH = pl.DeviceIdType.MESH
DELTA = (0, 1, 3, 2)


def kernel(a_hbm, out_ref, full, chunk, part, sum1, sum2, mine, theirs, ssem, rsem, lsem):
    kk, p = lax.axis_index("kk"), lax.axis_index("g")
    z, y = kk // 4, kk % 4
    rows, cols = a_hbm.shape
    quarter, half, strip = rows // 4, rows // 8, rows // 16

    zp, zm = {"kk": (z + 1) % 4 * 4 + y}, {"kk": (z + 3) % 4 * 4 + y}
    yp, ym = {"kk": z * 4 + (y + 1) % 4}, {"kk": z * 4 + (y + 3) % 4}
    gp, gm = {"g": (p + 1) % 8}, {"g": (p + 7) % 8}
    far = {"g": (p + 4) % 8}
    odd = p % 2 == 1
    low = p < 4

    own = pltpu.make_async_copy(a_hbm, full.at[:, pl.ds(0, cols)], lsem)
    own.start()
    barrier = pltpu.get_barrier_semaphore()
    for dev in (zp, zm, yp, ym, gp, gm):
        pl.semaphore_signal(barrier, inc=1, device_id=dev, device_id_type=MESH)

    @pl.when(odd)
    def _():
        pl.semaphore_signal(barrier, inc=1, device_id=far, device_id_type=MESH)

    pl.semaphore_wait(barrier, 6 + p % 2)
    own.wait()

    count = [0]
    sent = []

    def slot():
        count[0] += 1
        return count[0] - 1

    def copy(src, dst, dev, idx=None):
        i = slot() if idx is None else idx
        return pltpu.make_async_remote_copy(
            src_ref=src, dst_ref=dst, send_sem=ssem.at[i], recv_sem=rsem.at[i],
            device_id=dev, device_id_type=MESH)

    def send(src, dst, dev):
        c = copy(src, dst, dev)
        c.start()
        sent.append(c)
        return c

    def q(d):
        return pl.multiple_of((z + d) % 4 * quarter, quarter)

    def shard(start, size, r):
        return full.at[pl.ds(start, size), pl.ds(r * cols, cols)]

    def zplus(start, size, r_src):
        return send(shard(start, size, r_src), shard(start, size, (r_src + 3) % 4), zp)

    def zminus(start, size, r_src):
        return send(shard(start, size, r_src), shard(start, size, (r_src + 1) % 4), zm)

    far_idx = [slot() for _ in range(4)]

    def piece(j, r):
        if j == 0:
            return shard(q(0), quarter, r)
        return chunk.at[j - 1, :, pl.ds(r * cols, cols)]

    def far_copy(j, r, dev):
        return copy(piece(j, r), piece(4, r), dev, far_idx[r])

    passed = {}

    def pass_on(j, r):
        passed[j, r] = send(piece(j, r), piece(j + 1, r), gm)
        if j == 0:
            @pl.when(odd & ~low)
            def _():
                far_copy(0, r, far).start()

    pass_on(0, 0)
    m1, p1 = zplus(q(1), quarter, 0), zminus(q(3), quarter, 0)
    m2, p2 = zplus(q(2), half, 0), zminus(q(2) + half, half, 0)
    m1.wait_recv()
    pass_on(0, 3)
    p1.wait_recv()
    pass_on(0, 1)
    m2.wait_recv()
    m3 = zplus(q(1), half, 3)
    p2.wait_recv()
    p3 = zminus(q(3) + half, half, 1)
    m4, p4 = zplus(q(2) + half, half, 0), zminus(q(2), half, 0)
    m9, p9 = zplus(q(0), quarter, 3), zminus(q(0), quarter, 1)
    m7, p7 = zplus(q(0), quarter, 0), zminus(q(0), quarter, 0)
    m5, p5 = zplus(q(3), quarter, 0), zminus(q(1), quarter, 0)

    def strip_rows(d):
        return pl.ds(pl.multiple_of((y + d) % 4 * strip, strip), strip)

    def product(j, d0, n):
        for d in range(d0, d0 + n):
            left = full[pl.ds(q(0), quarter), :] if j == 0 else chunk[j - 1]
            part[j, :, pl.ds(d * quarter, quarter)] = lax.dot_general(
                left, full[pl.ds(q(DELTA[d]), quarter), :],
                (((1,), (1,)), ((), ())), preferred_element_type=jnp.float32)

    def unit(j, d0, n):
        c0, width = d0 * quarter, n * quarter
        hw = width // 2
        u = {}
        lo, hi, whole = pl.ds(c0, hw), pl.ds(c0 + hw, hw), pl.ds(c0, width)
        land = pl.ds(c0 // 2, hw)
        u["a"] = copy(part.at[j, strip_rows(2), lo], sum1.at[0, j, :, land], yp)
        u["b"] = copy(part.at[j, strip_rows(2), hi], sum1.at[1, j, :, land], ym)
        u["c"] = copy(part.at[j, strip_rows(1), whole], sum2.at[0, j, :, whole], yp)
        u["d"] = copy(part.at[j, strip_rows(3), whole], sum2.at[1, j, :, whole], ym)

        def begin():
            product(j, d0, n)
            u["a"].start()
            u["b"].start()

        def middle():
            u["a"].wait_recv()
            part[j, strip_rows(1), lo] += sum1[0, j, :, land]
            u["c"].start()
            u["b"].wait_recv()
            part[j, strip_rows(3), hi] += sum1[1, j, :, land]
            u["d"].start()

        def end():
            u["c"].wait_recv()
            u["d"].wait_recv()
            total = part[j, strip_rows(0), whole] + sum2[0, j, :, whole] + sum2[1, j, :, whole]
            if j % 2 == 0:
                for d in range(d0, d0 + n):
                    out_ref[j, :, pl.ds(q(DELTA[d]), quarter)] = total[:, (d - d0) * quarter:(d - d0 + 1) * quarter]
            else:
                mine[j // 2, :, whole] = total
                u["e"] = send(mine.at[j // 2, :, whole], theirs.at[j // 2, :, whole], gm)

        def receive():
            u["e"].wait_recv()
            for d in range(d0, d0 + n):
                out_ref[j, :, pl.ds(q(DELTA[d]), quarter)] = theirs[j // 2, :, pl.ds(d * quarter, quarter)]

        def settle():
            for key in "abcd":
                u[key].wait_send()

        return dict(begin=begin, middle=middle, end=end, receive=receive, settle=settle)

    u00, u10 = unit(0, 0, 1), unit(1, 0, 1)
    u01, u11 = unit(0, 1, 2), unit(1, 1, 2)
    u20 = unit(2, 0, 3)
    u02, u12, u22 = unit(0, 3, 1), unit(1, 3, 1), unit(2, 3, 1)
    u30, u31 = unit(3, 0, 2), unit(3, 2, 2)
    u40, u41 = unit(4, 0, 2), unit(4, 2, 2)

    m3.wait_recv()
    p3.wait_recv()
    pass_on(0, 2)
    u00["begin"]()
    for r in (0, 3, 1, 2):
        passed[0, r].wait_recv()
        pass_on(1, r)
    u10["begin"]()
    u00["middle"]()
    m4.wait_recv()
    p4.wait_recv()
    m9.wait_recv()
    p9.wait_recv()
    m7.wait_recv()
    m8 = zplus(q(3), half, 3)
    p7.wait_recv()
    p8 = zminus(q(1) + half, half, 1)
    u10["middle"]()
    u01["begin"]()
    u11["begin"]()
    for r in (0, 3, 1, 2):
        passed[1, r].wait_recv()
        pass_on(2, r)
    u01["middle"]()
    u20["begin"]()
    u11["middle"]()
    u00["end"]()
    u10["end"]()
    m5.wait_recv()
    p5.wait_recv()
    u20["middle"]()
    m8.wait_recv()
    p8.wait_recv()
    u02["begin"]()
    u12["begin"]()
    u22["begin"]()
    for r in (0, 3, 1, 2):
        passed[2, r].wait_recv()

        @pl.when(odd & low)
        def _():
            far_copy(3, r, gm).start()

    u30["begin"]()
    u02["middle"]()
    u12["middle"]()
    u22["middle"]()
    u31["begin"]()
    u30["middle"]()
    u01["end"]()
    u11["end"]()
    u31["middle"]()

    @pl.when(low)
    def _():
        for r in (0, 3, 1, 2):
            far_copy(0, r, far).wait_recv()
        u40["begin"]()
        u41["begin"]()

    u20["end"]()
    u02["end"]()
    u12["end"]()
    u22["end"]()

    @pl.when(low)
    def _():
        u40["middle"]()
        u41["middle"]()

    u30["end"]()
    u31["end"]()
    for u in (u10, u11, u12):
        u["receive"]()

    @pl.when(low)
    def _():
        u40["end"]()
        u41["end"]()

    @pl.when(~low)
    def _():
        out_ref[4] = jnp.zeros(out_ref.shape[1:], out_ref.dtype)

    u30["receive"]()
    u31["receive"]()

    for c in sent:
        c.wait_send()
    for u in (u00, u10, u01, u11, u20, u02, u12, u22, u30, u31):
        u["settle"]()

    @pl.when(low)
    def _():
        u40["settle"]()
        u41["settle"]()

    @pl.when(odd)
    def _():
        for r in range(4):
            far_copy(0, r, far).wait_send()


def solution(mesh):
    def local_fn(a_blk):
        rows, cols = a_blk.shape
        strip = rows // 16
        out = pl.pallas_call(
            kernel,
            out_shape=jax.ShapeDtypeStruct((5, strip, rows), jnp.float32),
            in_specs=[pl.BlockSpec(memory_space=pltpu.HBM)],
            out_specs=pl.BlockSpec(memory_space=pltpu.VMEM),
            scratch_shapes=[
                pltpu.VMEM((rows, 4 * cols), jnp.bfloat16),
                pltpu.VMEM((4, rows // 4, 4 * cols), jnp.bfloat16),
                pltpu.VMEM((5, rows // 4, rows), jnp.float32),
                pltpu.VMEM((2, 5, strip, rows // 2), jnp.float32),
                pltpu.VMEM((2, 5, strip, rows), jnp.float32),
                pltpu.VMEM((2, strip, rows), jnp.float32),
                pltpu.VMEM((2, strip, rows), jnp.float32),
                pltpu.SemaphoreType.DMA((112,)),
                pltpu.SemaphoreType.DMA((112,)),
                pltpu.SemaphoreType.DMA,
            ],
            compiler_params=pltpu.CompilerParams(
                collective_id=0, has_side_effects=True, vmem_limit_bytes=48 * 1024 * 1024),
        )(a_blk)
        return out[None]

    return jax.shard_map(local_fn, mesh=mesh, in_specs=(P(("m", "g"), "kk"),), out_specs=P(("m", "g"), None, "kk", None), check_vma=False)
```

time: 251 us -> 83.2 us (0.33)
  waiting for transfers between devices: 185 us -> 0 us
  Pallas kernels: 0 us -> 80.3 us
  other arithmetic: 16.9 us -> 0 us
  local copies, waits for them, and re-layouts: 16.4 us -> 2.28 us
  between operations: 13.4 us -> 0.01 us
  matrix products: 13.1 us -> 0 us
  starting transfers between devices: 5.11 us -> 0 us
    reduce_scatter x1 -> x0, waiting for transfers between devices: 144 us -> none  [local_fn(): result = lax.psum_scatter(result, 'kk', scatter_dimension=1, tiled=True)]
    pallas_call x0 -> x1, Pallas kernels: none -> 80.3 us  [local_fn(): pl.pallas_call(kernel, out_shape=jax.ShapeDtypeStruct((5, strip, rows), j...]
    ppermute x3 -> x0, waiting for transfers between devices: 40.8 us -> none  [fetch_block(): return lax.ppermute(a_blk, 'g', perm_pairs)]
    select_n x1 -> x0, other arithmetic: 16.9 us -> none  [local_fn(): jnp.where((slot_ids == half_size) & (dev_pos >= half_size), 0.0, result)]
    transpose x1 -> x0, local copies, waits for them, and re-layouts: 16.4 us -> none  [local_fn(): jnp.einsum('jrk,isk->jirs', big_stack, small_stack, preferred_element_typ...]
    dot_general x2 -> x0, matrix products: 13.1 us -> none  [the longest x1 8.26 us: local_fn(): jnp.einsum('jrk,isk->jirs', big_stack, small_stack, preferred_element_typ...]
    ppermute x3 -> x0, starting transfers between devices: 5.11 us -> none  [fetch_block(): return lax.ppermute(a_blk, 'g', perm_pairs)]
  transfers between devices with their start and end apart: 4 -> 0, of which waited for: 4 -> 0; matrix products, arithmetic and copies ran while one was open for 2% -> 0% of each run, Pallas kernels for 0% -> 0%
where the time goes in v1:
time: 83.2 us; the launch traced here: 82.6 us
  Pallas kernels  80.3 us (97%)
  local copies, waits for them, and re-layouts  2.28 us (3%)
    pallas_call x1, Pallas kernels, local_fn(): pl.pallas_call(kernel, out_shape=jax.ShapeDtypeStruct((5, strip, rows), j...  80.3 us
    unnamed x3, local copies, waits for them, and re-layouts  2.28 us

profile of v1, /device:TPU:1, one launch (start us, length us, event | category | flops | bytes accessed | tf_op | source)
XLA Modules:
  0.0 82.6 jit_solution(14761614948295544899)
XLA Ops:
  0.0 0.0 copy-start
  0.0 1.2 %copy-done = bf16[1024,512]{1,0:T(8,128)(2,1)S(1)} copy-done((bf16[1024,512]{1,0:T(8,128)(2,1)S(1)}, bf16[1024,512]{1,0:T(8,128)(2,1)}, u32[]{:S(2)}) %copy-start) | copy-done | bytes 1048600
  1.2 80.3 %shard_map.17 = f32[5,64,1024]{2,1,0:T(8,128)S(1)} custom-call(bf16[1024,512]{1,0:T(8,128)(2,1)S(1)} %copy-done), custom_call_target="tpu_custom_call" | custom-call | tf_op jit(solution)/shard_map/pallas_call | solution.py:275
  81.6 1.1 %copy.3 = f32[1,5,64,1024]{3,2,1,0:T(8,128)} copy(f32[1,5,64,1024]{3,2,1,0:T(8,128)S(1)} %bitcast.1) | data formatting | bytes 2621440
Async XLA Ops:
  0.0 1.2 %copy-start = (bf16[1024,512]{1,0:T(8,128)(2,1)S(1)}, bf16[1024,512]{1,0:T(8,128)(2,1)}, u32[]{:S(2)}) copy-start(bf16[1024,512]{1,0:T(8,128)(2,1)} %a_hbm.1) | copy-start | bytes 3145732

commit v2 on v0

v2 whole, which is shorter than its diff:
```python
import functools
import jax
import jax.numpy as jnp
from jax import lax
from jax.experimental import pallas as pl
from jax.experimental.pallas import tpu as pltpu
from jax.sharding import PartitionSpec as P

MESH = pl.DeviceIdType.MESH
DELTA = (0, 1, 3, 2)


def kernel(a_hbm, out_ref, full, chunk, part, sum1, sum2, mine, theirs, ssem, rsem, lsem, gate):
    kk, p = lax.axis_index("kk"), lax.axis_index("g")
    z, y = kk // 4, kk % 4
    rows, cols = a_hbm.shape
    quarter, half, strip = rows // 4, rows // 8, rows // 16

    zp, zm = {"kk": (z + 1) % 4 * 4 + y}, {"kk": (z + 3) % 4 * 4 + y}
    yp, ym = {"kk": z * 4 + (y + 1) % 4}, {"kk": z * 4 + (y + 3) % 4}
    gp, gm = {"g": (p + 1) % 8}, {"g": (p + 7) % 8}
    next_chip, last_chip = {"g": (p + 2) % 8}, {"g": (p + 6) % 8}
    odd = p % 2 == 1
    low = p < 4

    own = pltpu.make_async_copy(a_hbm, full.at[:, pl.ds(0, cols)], lsem)
    own.start()
    barrier = pltpu.get_barrier_semaphore()
    for dev in (zp, zm, yp, ym, gp, gm):
        pl.semaphore_signal(barrier, inc=1, device_id=dev, device_id_type=MESH)

    @pl.when(odd)
    def _():
        pl.semaphore_signal(barrier, inc=1, device_id=next_chip, device_id_type=MESH)
        pl.semaphore_signal(barrier, inc=1, device_id=last_chip, device_id_type=MESH)

    pl.semaphore_wait(barrier, 6 + p % 2 * 2)
    own.wait()

    slots = iter(range(ssem.shape[0]))

    def copy(src, dst, dev):
        i = next(slots)
        return pltpu.make_async_remote_copy(
            src_ref=src, dst_ref=dst, send_sem=ssem.at[i], recv_sem=rsem.at[i],
            device_id=dev, device_id_type=MESH)

    def start(*copies):
        for c in copies:
            c.start()

    def arrived(*copies):
        for c in copies:
            c.wait_recv()

    def left(*copies):
        for c in copies:
            c.wait_send()

    def q(d):
        return pl.multiple_of((z + d) % 4 * quarter, quarter)

    def shard(first, size, r):
        return full.at[pl.ds(first, size), pl.ds(r * cols, cols)]

    def zplus(first, size, r):
        return copy(shard(first, size, r), shard(first, size, (r + 3) % 4), zp)

    def zminus(first, size, r):
        return copy(shard(first, size, r), shard(first, size, (r + 1) % 4), zm)

    m1, p1 = zplus(q(1), quarter, 0), zminus(q(3), quarter, 0)
    m2, p2 = zplus(q(2), half, 0), zminus(q(2) + half, half, 0)
    m3, p3 = zplus(q(1), half, 3), zminus(q(3) + half, half, 1)
    m4, p4 = zplus(q(2) + half, half, 0), zminus(q(2), half, 0)
    m9, p9 = zplus(q(0), quarter, 3), zminus(q(0), quarter, 1)
    m7, p7 = zplus(q(0), quarter, 0), zminus(q(0), quarter, 0)
    m5, p5 = zplus(q(3), quarter, 0), zminus(q(1), quarter, 0)
    m8, p8 = zplus(q(3), half, 3), zminus(q(1) + half, half, 1)

    def piece(j, r):
        return shard(q(0), quarter, r) if j == 0 else chunk.at[j - 1, :, pl.ds(r * cols, cols)]

    def leg(src, dst, dev):
        return [copy(piece(src, r), piece(dst, r), dev) for r in range(4)]

    x1, x2, x3 = leg(0, 1, gm), leg(1, 2, gm), leg(2, 3, gm)
    y1, y2, x4 = leg(0, 5, next_chip), leg(5, 4, next_chip), leg(3, 4, gm)
    ARRIVAL = (0, 3, 1, 2)

    def own_piece(r):
        x1[r].start()

        @pl.when(odd)
        def _():
            y1[r].start()

    def forward(got, give, shards=ARRIVAL):
        for r in shards:
            got[r].wait_recv()
            give[r].start()

    def strip_rows(d):
        return pl.ds(pl.multiple_of((y + d) % 4 * strip, strip), strip)

    class Unit:
        def __init__(self, j, d0, n):
            step = half if j == 4 else quarter
            c0, width = d0 * step, n * step
            hw = width // 2
            self.j, self.ds, self.step = j, range(d0, d0 + n), step
            self.lo, self.hi, self.whole = pl.ds(c0, hw), pl.ds(c0 + hw, hw), pl.ds(c0, width)
            self.land = pl.ds(c0 // 2, hw)
            self.a = copy(part.at[j, strip_rows(2), self.lo], sum1.at[0, j, :, self.land], yp)
            self.b = copy(part.at[j, strip_rows(2), self.hi], sum1.at[1, j, :, self.land], ym)
            self.c = copy(part.at[j, strip_rows(1), self.whole], sum2.at[0, j, :, self.whole], yp)
            self.d = copy(part.at[j, strip_rows(3), self.whole], sum2.at[1, j, :, self.whole], ym)
            if j == 4:
                self.sends = [
                    copy(mine.at[2, :, pl.ds(d * step, step)], theirs.at[2, :, pl.ds(d * step, step)],
                         {"kk": (z + DELTA[d]) % 4 * 4 + y, "g": (p + 4) % 8})
                    for d in self.ds]
            elif j % 2:
                self.sends = [copy(mine.at[j // 2, :, self.whole], theirs.at[j // 2, :, self.whole], gm)]
            else:
                self.sends = []

        def multiply(self, d, lhs, rhs):
            part[self.j, :, pl.ds(d * self.step, self.step)] = lax.dot_general(
                lhs, rhs, (((1,), (1,)), ((), ())), preferred_element_type=jnp.float32)

        def begin(self):
            j = self.j
            for d in self.ds:
                rows_d = pl.ds(q(DELTA[d]), quarter)
                if j == 0:
                    self.multiply(d, full[pl.ds(q(0), quarter), :], full[rows_d, :])
                elif j < 4:
                    self.multiply(d, chunk[j - 1], full[rows_d, :])
                else:
                    @pl.when(low)
                    def _():
                        self.multiply(d, chunk[3], full[pl.ds(q(DELTA[d]), half), :])

                    @pl.when(~low)
                    def _():
                        self.multiply(d, full[rows_d, :], chunk[3, half:])
            start(self.a, self.b)

        def middle(self):
            j = self.j
            self.a.wait_recv()
            part[j, strip_rows(1), self.lo] += sum1[0, j, :, self.land]
            self.c.start()
            self.b.wait_recv()
            part[j, strip_rows(3), self.hi] += sum1[1, j, :, self.land]
            self.d.start()

        def place(self, value):
            for i, d in enumerate(self.ds):
                out_ref[self.j, :, pl.ds(q(DELTA[d]), self.step)] = value[:, i * self.step:(i + 1) * self.step]

        def end(self):
            j = self.j
            arrived(self.c, self.d)
            total = part[j, strip_rows(0), self.whole] + sum2[0, j, :, self.whole] + sum2[1, j, :, self.whole]
            if j == 4:
                @pl.when(low)
                def _():
                    self.place(total)

                @pl.when(~low)
                def _():
                    mine[2, :, self.whole] = total
                    start(*self.sends)
            elif j % 2:
                mine[j // 2, :, self.whole] = total
                start(*self.sends)
            else:
                self.place(total)

        def receive(self):
            arrived(*self.sends)
            if self.j == 4:
                for d in self.ds:
                    first = pl.multiple_of(q(4 - DELTA[d]) + half, half)
                    out_ref[4, :, pl.ds(first, half)] = theirs[2, :, pl.ds(d * half, half)]
            else:
                self.place(theirs[self.j // 2, :, self.whole])

        def settle(self):
            left(self.a, self.b, self.c, self.d)
            if self.j != 4:
                left(*self.sends)

    u00, u10 = Unit(0, 0, 1), Unit(1, 0, 1)
    u01, u11 = Unit(0, 1, 1), Unit(1, 1, 1)
    u20, u21 = Unit(2, 0, 1), Unit(2, 1, 1)
    u02, u12, u22 = Unit(0, 2, 1), Unit(1, 2, 1), Unit(2, 2, 1)
    u03, u13, u23 = Unit(0, 3, 1), Unit(1, 3, 1), Unit(2, 3, 1)
    u30, u31 = Unit(3, 0, 2), Unit(3, 2, 2)
    u40, u41 = Unit(4, 0, 2), Unit(4, 2, 2)
    always = (u00, u10, u01, u11, u20, u21, u02, u12, u22, u03, u13, u23, u30, u31, u40, u41)

    def both(*steps):
        for step in steps:
            step()

    rest = (m9, p9, m7, p4, m5, p5)

    def head():
        start(m2, p2, m1, p1)
        own_piece(0)
        arrived(m2)
        start(m3)
        arrived(p2)
        start(p3)
        pl.when(~odd)(lambda: start(m4, p7))
        forward(x1, x2, shards=(0,))
        arrived(m1)
        own_piece(3)
        arrived(p1)
        own_piece(1)
        pl.when(~odd)(lambda: start(*rest))
        arrived(m3, p3)
        own_piece(2)
        u00.begin()

    def even_core():
        forward(x1, x2, shards=(3, 1, 2))
        u10.begin()
        arrived(m4, p7)
        start(p8)
        arrived(p9)
        both(u01.begin, u11.begin, u00.middle, u10.middle)
        forward(x2, x3, shards=(0, 3))
        arrived(m9, m7)
        start(m8)
        arrived(p4)
        pl.semaphore_signal(gate, inc=1, device_id=gp, device_id_type=MESH)
        both(u02.begin, u12.begin)
        forward(x2, x3, shards=(1, 2))
        both(u20.begin, u21.begin, u22.begin, u01.middle, u11.middle, u02.middle, u12.middle)
        arrived(m5, p5, m8, p8)
        both(u03.begin, u13.begin, u23.begin, u20.middle, u21.middle, u22.middle)
        arrived(*x3)
        both(u30.begin, u31.begin, u03.middle, u13.middle, u23.middle)
        both(u10.end, u11.end, u00.end, u01.end, u30.middle, u31.middle, u12.end)
        arrived(*x4)
        both(u40.begin, u41.begin)
        both(u02.end, u20.end, u21.end, u22.end, u13.end)
        both(u40.middle, u41.middle)
        both(u30.end, u31.end, u40.end, u41.end, u03.end, u23.end)

    def odd_core():
        forward(x1, x2, shards=(3, 1))
        forward(y1, y2, shards=(0, 3))
        pl.semaphore_wait(gate, 1)
        start(m4, p7, *rest)
        forward(x1, x2, shards=(2,))
        both(u10.begin, u00.middle)
        forward(y1, y2, shards=(1, 2))
        u10.middle()
        forward(x2, x3, shards=(0, 3, 1))
        arrived(m4, p7)
        start(p8)
        arrived(p9)
        both(u01.begin, u11.begin)
        forward(x2, x3, shards=(2,))
        both(u20.begin, u21.begin)
        arrived(m9, m7)
        start(m8)
        arrived(p4)
        both(u02.begin, u12.begin, u22.begin, u01.middle, u11.middle, u20.middle, u21.middle)
        arrived(m5, p5, m8, p8, *y2)
        both(u40.begin, u41.begin, u03.begin, u13.begin, u23.begin)
        both(u02.middle, u12.middle, u22.middle, u40.middle, u41.middle)
        forward(x3, x4)
        both(u30.begin, u31.begin, u13.middle, u03.middle, u23.middle)
        both(u10.end, u11.end, u00.end, u01.end, u20.end, u21.end, u12.end, u30.middle, u31.middle)
        both(u40.end, u41.end, u13.end, u02.end, u22.end, u03.end, u23.end, u30.end, u31.end)

    head()
    pl.when(~odd)(even_core)
    pl.when(odd)(odd_core)
    both(u10.receive, u11.receive, u12.receive, u13.receive, u30.receive, u31.receive)

    @pl.when(low)
    def _():
        both(u40.receive, u41.receive)

    @pl.when(~low)
    def _():
        out_ref[4] = jnp.zeros(out_ref.shape[1:], out_ref.dtype)

    left(m1, p1)
    left(m2, p2, m3, p3, m4, p4, m5, p5, m7, p7, m8, p8, m9, p9, *x1, *x2, *x3)
    for u in always:
        u.settle()

    @pl.when(odd)
    def _():
        left(*x4, *y1, *y2)

    @pl.when(~low)
    def _():
        left(*u40.sends, *u41.sends)


def solution(mesh):
    def local_fn(a_blk):
        rows, cols = a_blk.shape
        strip = rows // 16
        out = pl.pallas_call(
            kernel,
            out_shape=jax.ShapeDtypeStruct((5, strip, rows), jnp.float32),
            in_specs=[pl.BlockSpec(memory_space=pltpu.HBM)],
            out_specs=pl.BlockSpec(memory_space=pltpu.VMEM),
            scratch_shapes=[
                pltpu.VMEM((rows, 4 * cols), jnp.bfloat16),
                pltpu.VMEM((5, rows // 4, 4 * cols), jnp.bfloat16),
                pltpu.VMEM((5, rows // 4, rows), jnp.float32),
                pltpu.VMEM((2, 5, strip, rows // 2), jnp.float32),
                pltpu.VMEM((2, 5, strip, rows), jnp.float32),
                pltpu.VMEM((3, strip, rows), jnp.float32),
                pltpu.VMEM((3, strip, rows), jnp.float32),
                pltpu.SemaphoreType.DMA((160,)),
                pltpu.SemaphoreType.DMA((160,)),
                pltpu.SemaphoreType.DMA,
                pltpu.SemaphoreType.REGULAR,
            ],
            compiler_params=pltpu.CompilerParams(
                collective_id=0, has_side_effects=True, vmem_limit_bytes=48 * 1024 * 1024),
        )(a_blk)
        return out[None]

    return jax.shard_map(local_fn, mesh=mesh, in_specs=(P(("m", "g"), "kk"),), out_specs=P(("m", "g"), None, "kk", None), check_vma=False)
```

time: 251 us -> 74.8 us (0.30)
  the two profiles are of different devices: /device:TPU:1 before, /device:TPU:0 now
where the time goes in v2:
time: 74.8 us; the launch traced here: 74.7 us
  Pallas kernels  72.4 us (97%)
  local copies, waits for them, and re-layouts  2.28 us (3%)
    pallas_call x1, Pallas kernels, local_fn(): pl.pallas_call(kernel, out_shape=jax.ShapeDtypeStruct((5, strip, rows), j...  72.4 us
    unnamed x3, local copies, waits for them, and re-layouts  2.28 us

profile of v2, /device:TPU:0, one launch (start us, length us, event | category | flops | bytes accessed | tf_op | source)
XLA Modules:
  0.0 74.7 jit_solution(1285854683284714179)
XLA Ops:
  0.0 0.0 copy-start
  0.0 1.2 %copy-done = bf16[1024,512]{1,0:T(8,128)(2,1)S(1)} copy-done((bf16[1024,512]{1,0:T(8,128)(2,1)S(1)}, bf16[1024,512]{1,0:T(8,128)(2,1)}, u32[]{:S(2)}) %copy-start) | copy-done | bytes 1048600
  1.2 72.4 %shard_map.17 = f32[5,64,1024]{2,1,0:T(8,128)S(1)} custom-call(bf16[1024,512]{1,0:T(8,128)(2,1)S(1)} %copy-done), custom_call_target="tpu_custom_call" | custom-call | tf_op jit(solution)/shard_map/pallas_call | solution.py:314
  73.6 1.1 %copy.3 = f32[1,5,64,1024]{3,2,1,0:T(8,128)} copy(f32[1,5,64,1024]{3,2,1,0:T(8,128)S(1)} %bitcast.1) | data formatting | bytes 2621440
Async XLA Ops:
  0.0 1.2 %copy-start = (bf16[1024,512]{1,0:T(8,128)(2,1)S(1)}, bf16[1024,512]{1,0:T(8,128)(2,1)}, u32[]{:S(2)}) copy-start(bf16[1024,512]{1,0:T(8,128)(2,1)} %a_hbm.1) | copy-start | bytes 3145732

commit v3 on v2

v3 whole, which is shorter than its diff:
```python
import functools
import jax
import jax.numpy as jnp
from jax import lax
from jax.experimental import pallas as pl
from jax.experimental.pallas import tpu as pltpu
from jax.sharding import PartitionSpec as P

MESH = pl.DeviceIdType.MESH
DELTA = (0, 1, 3, 2)


def kernel(a_hbm, a_strips, out_ref, full, fully, chunk, chunky, part, sum1, sum2, mine, theirs, ssem, rsem, lsem, lsem2, gate):
    kk, p = lax.axis_index("kk"), lax.axis_index("g")
    z, y = kk // 4, kk % 4
    rows, cols = a_hbm.shape
    quarter, half, strip = rows // 4, rows // 8, rows // 16

    zp, zm = {"kk": (z + 1) % 4 * 4 + y}, {"kk": (z + 3) % 4 * 4 + y}
    yp, ym = {"kk": z * 4 + (y + 1) % 4}, {"kk": z * 4 + (y + 3) % 4}
    gp, gm = {"g": (p + 1) % 8}, {"g": (p + 7) % 8}
    next_chip, last_chip = {"g": (p + 2) % 8}, {"g": (p + 6) % 8}
    odd = p % 2 == 1
    low = p < 4

    own = pltpu.make_async_copy(a_hbm, full.at[:, pl.ds(0, cols)], lsem)
    own.start()
    own_too = pltpu.make_async_copy(a_strips, fully.at[:, :, :, pl.ds(0, cols)], lsem2)
    pl.when(odd)(own_too.start)
    barrier = pltpu.get_barrier_semaphore()
    for dev in (zp, zm, yp, ym, gp, gm):
        pl.semaphore_signal(barrier, inc=1, device_id=dev, device_id_type=MESH)

    @pl.when(odd)
    def _():
        pl.semaphore_signal(barrier, inc=1, device_id=next_chip, device_id_type=MESH)
        pl.semaphore_signal(barrier, inc=1, device_id=last_chip, device_id_type=MESH)

    pl.semaphore_wait(barrier, 6 + p % 2 * 2)
    own.wait()
    pl.when(odd)(own_too.wait)

    slots = iter(range(ssem.shape[0]))

    def copy(src, dst, dev):
        i = next(slots)
        return pltpu.make_async_remote_copy(
            src_ref=src, dst_ref=dst, send_sem=ssem.at[i], recv_sem=rsem.at[i],
            device_id=dev, device_id_type=MESH)

    def start(*copies):
        for c in copies:
            c.start()

    def arrived(*copies):
        for c in copies:
            c.wait_recv()

    def left(*copies):
        for c in copies:
            c.wait_send()

    def q(d):
        return pl.multiple_of((z + d) % 4 * quarter, quarter)

    def shard(first, size, r):
        return full.at[pl.ds(first, size), pl.ds(r * cols, cols)]

    def zplus(first, size, r):
        return copy(shard(first, size, r), shard(first, size, (r + 3) % 4), zp)

    def zminus(first, size, r):
        return copy(shard(first, size, r), shard(first, size, (r + 1) % 4), zm)

    m1, p1 = [zplus(q(1) + h, half, 0) for h in (0, half)], [zminus(q(3) + h, half, 0) for h in (0, half)]
    m2, p2 = zplus(q(2), half, 0), zminus(q(2) + half, half, 0)
    m3, p3 = zplus(q(1), half, 3), zminus(q(3) + half, half, 1)
    m4, p4 = zplus(q(2) + half, half, 0), zminus(q(2), half, 0)
    m9, p9 = zplus(q(0), quarter, 3), zminus(q(0), quarter, 1)
    m7, p7 = zplus(q(0), quarter, 0), zminus(q(0), quarter, 0)
    m5, p5 = zplus(q(3), quarter, 0), zminus(q(1), quarter, 0)
    m8, p8 = zplus(q(3), half, 3), zminus(q(1) + half, half, 1)

    def piece(j, r, first=0, size=quarter):
        if j == 0:
            return shard(q(0) + first, size, r)
        return chunk.at[j - 1, pl.ds(first, size), pl.ds(r * cols, cols)]

    def leg(src, dst, dev):
        return [copy(piece(src, r), piece(dst, r), dev) for r in range(4)]

    def halves(dst, dev):
        return [[copy(piece(0, r, h, half), piece(dst, r, h, half), dev) for h in (0, half)] for r in range(4)]

    x1, x2, x3 = halves(1, gm), leg(1, 2, gm), leg(2, 3, gm)
    x4 = leg(3, 4, gm)
    ARRIVAL = (0, 3, 1, 2)

    def own_piece(r, h):
        x1[r][h].start()

    def yshard(first, r):
        return fully.at[pl.ds(first, 2), :, :, pl.ds(r * cols, cols)]

    def yplus(first, r):
        return copy(yshard(first, r), yshard(first, (r + 3) % 4), yp)

    def yminus(first, r):
        return copy(yshard(first, r), yshard(first, (r + 1) % 4), ym)

    g1, h1, g2, h2 = yplus(0, 0), yminus(2, 0), yplus(2, 0), yminus(0, 0)
    g3, h3 = yplus(0, 3), yminus(2, 1)

    def ypiece(where, r):
        at = pl.ds(r * cols, cols)
        return fully.at[:, y, :, at] if where < 0 else chunky.at[where, :, :, at]

    y1 = [copy(ypiece(-1, r), ypiece(0, r), next_chip) for r in range(4)]
    y2 = [copy(ypiece(0, r), ypiece(1, r), next_chip) for r in range(4)]

    def forward(got, give, shards=ARRIVAL):
        for r in shards:
            arrived(*(got[r] if isinstance(got[r], list) else (got[r],)))
            give[r].start()

    class Unit:
        def __init__(self, j, d0, n, turned=False):
            step = half if j == 4 else quarter
            c0, width = d0 * step, n * step
            hw = width // 2
            self.j, self.ds, self.step, self.turned = j, range(d0, d0 + n), step, turned
            plus, minus, self.at = (zp, zm, z) if turned else (yp, ym, y)
            self.lo, self.hi, self.whole = pl.ds(c0, hw), pl.ds(c0 + hw, hw), pl.ds(c0, width)
            self.land = pl.ds(c0 // 2, hw)
            self.a = copy(part.at[j, self.strip(2), self.lo], sum1.at[0, j, :, self.land], plus)
            self.b = copy(part.at[j, self.strip(2), self.hi], sum1.at[1, j, :, self.land], minus)
            self.c = copy(part.at[j, self.strip(1), self.whole], sum2.at[0, j, :, self.whole], plus)
            self.d = copy(part.at[j, self.strip(3), self.whole], sum2.at[1, j, :, self.whole], minus)
            if j == 4:
                self.sends = [
                    copy(mine.at[2, :, pl.ds(d * step, step)], theirs.at[2, :, pl.ds(d * step, step)],
                         {"kk": z * 4 + (y + d) % 4 if turned else (z + DELTA[d]) % 4 * 4 + y, "g": (p + 4) % 8})
                    for d in self.ds]
            elif j % 2:
                self.sends = [copy(mine.at[j // 2, :, self.whole], theirs.at[j // 2, :, self.whole], gm)]
            else:
                self.sends = []

        def strip(self, d):
            return pl.ds(pl.multiple_of((self.at + d) % 4 * strip, strip), strip)

        def multiply(self, d, lhs, rhs):
            lhs, rhs = (v.reshape(-1, v.shape[-1]) for v in (lhs, rhs))
            part[self.j, :, pl.ds(d * self.step, rhs.shape[0])] = lax.dot_general(
                lhs, rhs, (((1,), (1,)), ((), ())), preferred_element_type=jnp.float32)

        def begin(self):
            j = self.j
            if self.turned:
                self.begin_turned()
            elif j < 4:
                for d in self.ds:
                    rows_j = full[pl.ds(q(0), quarter), :] if j == 0 else chunk[j - 1]
                    self.multiply(d, rows_j, full[pl.ds(q(DELTA[d]), quarter), :])
            else:
                @pl.when(low)
                def _():
                    for d in self.ds:
                        self.multiply(d, chunk[3], full[pl.ds(q(DELTA[d]), half), :])

                @pl.when(~low)
                def _():
                    for d in self.ds:
                        self.multiply(d, full[pl.ds(q(DELTA[d]), quarter), :], chunk[3, half:])
            start(self.a, self.b)

        def begin_turned(self):
            if self.j == 0:
                for d in self.ds:
                    self.multiply(d, fully[:, y], fully[d])
            else:
                @pl.when(low)
                def _():
                    self.multiply(self.ds[0], chunky[1], fully[self.ds[0] // 2])

                @pl.when(~low)
                def _():
                    for d in self.ds:
                        self.multiply(d, fully[:, (y + d) % 4], chunky[1, 2:])

        def middle(self):
            j = self.j
            self.a.wait_recv()
            part[j, self.strip(1), self.lo] += sum1[0, j, :, self.land]
            self.c.start()
            self.b.wait_recv()
            part[j, self.strip(3), self.hi] += sum1[1, j, :, self.land]
            self.d.start()

        def place(self, value):
            if self.turned:
                out_ref[self.j, :, self.whole] = value
                return
            for i, d in enumerate(self.ds):
                out_ref[self.j, :, pl.ds(q(DELTA[d]), self.step)] = value[:, i * self.step:(i + 1) * self.step]

        def end(self):
            j = self.j
            arrived(self.c, self.d)
            total = part[j, self.strip(0), self.whole] + sum2[0, j, :, self.whole] + sum2[1, j, :, self.whole]
            if j == 4:
                @pl.when(low)
                def _():
                    self.place(total)

                @pl.when(~low)
                def _():
                    mine[2, :, self.whole] = total
                    start(*self.sends)
            elif j % 2:
                mine[j // 2, :, self.whole] = total
                start(*self.sends)
            else:
                self.place(total)

        def receive(self):
            arrived(*self.sends)
            if self.j == 4:
                for d in self.ds:
                    first = pl.multiple_of(q(4 - DELTA[d]) + half, half)
                    out_ref[4, :, pl.ds(first, half)] = theirs[2, :, pl.ds(d * half, half)]
            else:
                self.place(theirs[self.j // 2, :, self.whole])

        def settle(self):
            left(self.a, self.b, self.c, self.d)
            if self.j != 4:
                left(*self.sends)

    u00, u10 = Unit(0, 0, 1), Unit(1, 0, 1)
    u01, u11 = Unit(0, 1, 1), Unit(1, 1, 1)
    u20, u21 = Unit(2, 0, 1), Unit(2, 1, 1)
    u02, u12, u22 = Unit(0, 2, 1), Unit(1, 2, 1), Unit(2, 2, 1)
    u03, u13, u23 = Unit(0, 3, 1), Unit(1, 3, 1), Unit(2, 3, 1)
    u30, u31 = Unit(3, 0, 2), Unit(3, 2, 2)
    u40, u41 = Unit(4, 0, 2), Unit(4, 2, 2)
    v00, v01 = Unit(0, 0, 2, turned=True), Unit(0, 2, 2, turned=True)
    v40, v41 = Unit(4, 0, 2, turned=True), Unit(4, 2, 2, turned=True)
    always = (u10, u11, u20, u21, u12, u22, u13, u23, u30, u31)
    even_only, odd_only = (u00, u01, u02, u03, u40, u41), (v00, v01, v40, v41)

    def receive_turned():
        arrived(*v40.sends, *v41.sends)
        cols_of = [theirs[2, :, pl.ds(pl.multiple_of((y + 4 - i) % 4 * half, half), half)] for i in range(4)]
        out_ref[4, :, pl.ds(2 * quarter, quarter)] = jnp.concatenate([v[:, :strip] for v in cols_of], axis=1)
        out_ref[4, :, pl.ds(3 * quarter, quarter)] = jnp.concatenate([v[:, strip:] for v in cols_of], axis=1)

    def both(*steps):
        for step in steps:
            step()

    rest = (m9, p9, m7, p4, m5, p5)

    def head(is_odd):
        start(m2, p2)
        if not is_odd:
            start(m1[0], p1[0], m1[1], p1[1])
        own_piece(0, 0)
        own_piece(0, 1)
        if is_odd:
            start(g1, h1, g2, h2, y1[0])
        arrived(m2)
        start(m3)
        arrived(p2)
        start(p3)
        if is_odd:
            start(m1[0], p1[0], m1[1], p1[1])
        else:
            start(m4, p7)
        forward(x1, x2, shards=(0,))
        if is_odd:
            arrived(g1)
            start(g3)
            arrived(h1)
            start(h3)
        for h in (0, 1):
            arrived(m1[h])
            own_piece(3, h)
            arrived(p1[h])
            own_piece(1, h)
        if not is_odd:
            start(*rest)
        arrived(m3)
        own_piece(2, 0)
        arrived(p3)
        own_piece(2, 1)

    def even_core():
        head(False)
        u00.begin()
        forward(x1, x2, shards=(3, 1, 2))
        u10.begin()
        arrived(m4, p7)
        start(p8)
        arrived(p9)
        both(u01.begin, u11.begin, u00.middle, u10.middle)
        forward(x2, x3, shards=(0, 3))
        arrived(m9, m7)
        start(m8)
        arrived(p4)
        pl.semaphore_signal(gate, inc=1, device_id=gp, device_id_type=MESH)
        both(u02.begin, u12.begin, u01.middle, u11.middle)
        forward(x2, x3, shards=(1, 2))
        both(u20.begin, u21.begin, u22.begin, u12.middle, u02.middle)
        arrived(m5, p5, m8, p8)
        both(u03.begin, u13.begin, u23.begin, u20.middle, u21.middle, u22.middle)
        arrived(*x3)
        both(u30.begin, u31.begin)
        both(u13.middle, u03.middle, u10.end, u11.end, u00.end, u01.end, u30.middle, u31.middle, u12.end)
        arrived(*x4)
        both(u40.begin, u41.begin, u23.middle)
        both(u13.end, u02.end, u20.end, u21.end, u22.end)
        both(u40.middle, u41.middle)
        both(u30.end, u31.end, u40.end, u41.end, u03.end, u23.end)

    def odd_core():
        head(True)
        forward(x1, x2, shards=(3, 1))
        arrived(g2)
        start(y1[3])
        arrived(h2)
        start(y1[1])
        pl.semaphore_wait(gate, 1)
        start(m4, p7, *rest)
        forward(x1, x2, shards=(2,))
        u10.begin()
        arrived(g3, h3)
        start(y1[2])
        forward(x2, x3, shards=(0, 3))
        u10.middle()
        forward(x2, x3, shards=(1,))
        arrived(m4, p7)
        start(p8)
        arrived(p9)
        u11.begin()
        forward(x2, x3, shards=(2,))
        both(u20.begin, u21.begin)
        forward(y1, y2, shards=(0, 3, 1))
        arrived(m9, m7)
        start(m8)
        arrived(p4)
        both(u12.begin, u22.begin, u11.middle, u20.middle, u21.middle)
        forward(y1, y2, shards=(2,))
        arrived(m5, p5, m8, p8)
        both(u13.begin, u23.begin, v00.begin, v01.begin)
        forward(x3, x4, shards=(0, 3))
        both(u12.middle)
        forward(x3, x4, shards=(1, 2))
        both(u30.begin, u31.begin, u13.middle, v00.middle, v01.middle)
        arrived(*y2)
        both(v40.begin, v41.begin, u10.end, u11.end, u20.end, u21.end, u12.end)
        both(u30.middle, u31.middle, v40.middle, v41.middle, u22.middle, u23.middle)
        both(v00.end, v01.end, v40.end, v41.end, u13.end, u30.end, u31.end, u22.end, u23.end)

    pl.when(~odd)(even_core)
    pl.when(odd)(odd_core)
    both(u10.receive, u11.receive, u12.receive, u13.receive, u30.receive, u31.receive)

    @pl.when(low & ~odd)
    def _():
        both(u40.receive, u41.receive)

    @pl.when(low & odd)
    def _():
        receive_turned()

    @pl.when(~low)
    def _():
        out_ref[4] = jnp.zeros(out_ref.shape[1:], out_ref.dtype)

    left(*m1, *p1, m2, p2, m3, p3, m4, p4, m5, p5, m7, p7, m8, p8, m9, p9, *x2, *x3)
    for r in range(4):
        left(*x1[r])
    for u in always:
        u.settle()

    @pl.when(odd)
    def _():
        left(*x4, *y1, *y2, g1, h1, g2, h2, g3, h3)
        for u in odd_only:
            u.settle()

    @pl.when(~odd)
    def _():
        for u in even_only:
            u.settle()

    @pl.when(~low & odd)
    def _():
        left(*v40.sends, *v41.sends)

    @pl.when(~low & ~odd)
    def _():
        left(*u40.sends, *u41.sends)

def solution(mesh):
    def local_fn(a_blk):
        rows, cols = a_blk.shape
        strip = rows // 16
        out = pl.pallas_call(
            kernel,
            out_shape=jax.ShapeDtypeStruct((5, strip, rows), jnp.float32),
            in_specs=[pl.BlockSpec(memory_space=pltpu.HBM)] * 2,
            out_specs=pl.BlockSpec(memory_space=pltpu.VMEM),
            scratch_shapes=[
                pltpu.VMEM((rows, 4 * cols), jnp.bfloat16),
                pltpu.VMEM((4, 4, strip, 4 * cols), jnp.bfloat16),
                pltpu.VMEM((4, rows // 4, 4 * cols), jnp.bfloat16),
                pltpu.VMEM((2, 4, strip, 4 * cols), jnp.bfloat16),
                pltpu.VMEM((5, rows // 4, rows), jnp.float32),
                pltpu.VMEM((2, 5, strip, rows // 2), jnp.float32),
                pltpu.VMEM((2, 5, strip, rows), jnp.float32),
                pltpu.VMEM((3, strip, rows), jnp.float32),
                pltpu.VMEM((3, strip, rows), jnp.float32),
                pltpu.SemaphoreType.DMA((220,)),
                pltpu.SemaphoreType.DMA((220,)),
                pltpu.SemaphoreType.DMA,
                pltpu.SemaphoreType.DMA,
                pltpu.SemaphoreType.REGULAR,
            ],
            compiler_params=pltpu.CompilerParams(
                collective_id=0, has_side_effects=True, vmem_limit_bytes=48 * 1024 * 1024),
        )(pltpu.with_memory_space_constraint(a_blk, pltpu.HBM),
          pltpu.with_memory_space_constraint(a_blk.reshape(4, 4, strip, cols), pltpu.HBM))
        return out[None]

    return jax.shard_map(local_fn, mesh=mesh, in_specs=(P(("m", "g"), "kk"),), out_specs=P(("m", "g"), None, "kk", None), check_vma=False)
```

time: 74.8 us -> 70 us (0.936)
  the two profiles are of different devices: /device:TPU:0 before, /device:TPU:1 now
where the time goes in v3:
time: 70 us; the launch traced here: 68.8 us
  Pallas kernels  67.7 us (97%)
  local copies, waits for them, and re-layouts  1.06 us (2%)
    pallas_call x1, Pallas kernels, local_fn(): pl.pallas_call(kernel, out_shape=jax.ShapeDtypeStruct((5, strip, rows), j...  67.7 us

profile of v3, /device:TPU:1, one launch (start us, length us, event | category | flops | bytes accessed | tf_op | source)
XLA Modules:
  0.0 68.8 jit_solution(13850882442738744171)
XLA Ops:
  0.0 67.7 %shard_map.17 = f32[5,64,1024]{2,1,0:T(8,128)S(1)} custom-call(bf16[1024,512]{1,0:T(8,128)(2,1)} %a_hbm.1, bf16[4,4,64,512]{3,2,1,0:T(8,128)(2,1)} %bitcast.3), custom_call_target="tpu_custom_call" | custom-call | tf_op jit(solution)/shard_map/pallas_call | solution.py:410
  67.7 1.1 %copy.3 = f32[1,5,64,1024]{3,2,1,0:T(8,128)} copy(f32[1,5,64,1024]{3,2,1,0:T(8,128)S(1)} %bitcast.2) | data formatting | bytes 2621440

commit v4 on v3

--- a/solution.py
+++ b/solution.py
@@ -10,7 +10,7 @@
 DELTA = (0, 1, 3, 2)
 
 
-def kernel(a_hbm, a_strips, out_ref, full, fully, chunk, chunky, part, sum1, sum2, mine, theirs, ssem, rsem, lsem, lsem2, gate):
+def kernel(a_hbm, a_strips, out_ref, full, fully, chunk, chunky, spare, part, sum1, sum2, mine, theirs, ssem, rsem, lsem, lsem2, gate):
     kk, p = lax.axis_index("kk"), lax.axis_index("g")
     z, y = kk // 4, kk % 4
     rows, cols = a_hbm.shape
@@ -20,23 +20,24 @@
     yp, ym = {"kk": z * 4 + (y + 1) % 4}, {"kk": z * 4 + (y + 3) % 4}
     gp, gm = {"g": (p + 1) % 8}, {"g": (p + 7) % 8}
     next_chip, last_chip = {"g": (p + 2) % 8}, {"g": (p + 6) % 8}
+    across, behind = {"g": (p + 3) % 8}, {"g": (p + 5) % 8}
     odd = p % 2 == 1
     low = p < 4
+    relays = (p == 1) | (p == 7)
 
     own = pltpu.make_async_copy(a_hbm, full.at[:, pl.ds(0, cols)], lsem)
     own.start()
     own_too = pltpu.make_async_copy(a_strips, fully.at[:, :, :, pl.ds(0, cols)], lsem2)
     pl.when(odd)(own_too.start)
     barrier = pltpu.get_barrier_semaphore()
-    for dev in (zp, zm, yp, ym, gp, gm):
+    for dev in (zp, zm, yp, ym, gp, gm, next_chip, last_chip):
         pl.semaphore_signal(barrier, inc=1, device_id=dev, device_id_type=MESH)
 
     @pl.when(odd)
     def _():
-        pl.semaphore_signal(barrier, inc=1, device_id=next_chip, device_id_type=MESH)
-        pl.semaphore_signal(barrier, inc=1, device_id=last_chip, device_id_type=MESH)
-
-    pl.semaphore_wait(barrier, 6 + p % 2 * 2)
+        pl.semaphore_signal(barrier, inc=1, device_id=behind, device_id_type=MESH)
+
+    pl.semaphore_wait(barrier, 9 - p % 2)
     own.wait()
     pl.when(odd)(own_too.wait)
 
@@ -94,6 +95,8 @@
 
     x1, x2, x3 = halves(1, gm), leg(1, 2, gm), leg(2, 3, gm)
     x4 = leg(3, 4, gm)
+    w1 = {r: copy(piece(0, r), spare.at[:, pl.ds(i * cols, cols)], next_chip) for i, r in enumerate((0, 3))}
+    w2 = {r: copy(spare.at[:, pl.ds(i * cols, cols)], piece(3, r), across) for i, r in enumerate((0, 3))}
     ARRIVAL = (0, 3, 1, 2)
 
     def own_piece(r, h):
@@ -125,7 +128,8 @@
 
     class Unit:
         def __init__(self, j, d0, n, turned=False):
-            step = half if j == 4 else quarter
+            self.split = j == 4 and not turned
+            step = half if self.split else quarter
             c0, width = d0 * step, n * step
             hw = width // 2
             self.j, self.ds, self.step, self.turned = j, range(d0, d0 + n), step, turned
@@ -136,33 +140,26 @@
             self.b = copy(part.at[j, self.strip(2), self.hi], sum1.at[1, j, :, self.land], minus)
             self.c = copy(part.at[j, self.strip(1), self.whole], sum2.at[0, j, :, self.whole], plus)
             self.d = copy(part.at[j, self.strip(3), self.whole], sum2.at[1, j, :, self.whole], minus)
-            if j == 4:
-                self.sends = [
-                    copy(mine.at[2, :, pl.ds(d * step, step)], theirs.at[2, :, pl.ds(d * step, step)],
-                         {"kk": z * 4 + (y + d) % 4 if turned else (z + DELTA[d]) % 4 * 4 + y, "g": (p + 4) % 8})
-                    for d in self.ds]
+            self.sends = []
+            if self.split:
+                for d in self.ds:
+                    cols_d = pl.ds(d * step, step)
+                    dev = {"kk": (z + DELTA[d]) % 4 * 4 + y, "g": (p + 4) % 8}
+                    self.sends.append(copy(mine.at[2, :, cols_d], theirs.at[2, :, cols_d], dev))
             elif j % 2:
-                self.sends = [copy(mine.at[j // 2, :, self.whole], theirs.at[j // 2, :, self.whole], gm)]
-            else:
-                self.sends = []
+                self.sends.append(copy(mine.at[j // 2, :, self.whole], theirs.at[j // 2, :, self.whole], gm))
 
         def strip(self, d):
             return pl.ds(pl.multiple_of((self.at + d) % 4 * strip, strip), strip)
 
         def multiply(self, d, lhs, rhs):
             lhs, rhs = (v.reshape(-1, v.shape[-1]) for v in (lhs, rhs))
-            part[self.j, :, pl.ds(d * self.step, rhs.shape[0])] = lax.dot_general(
+            part[self.j, :, pl.ds(d * self.step, self.step)] = lax.dot_general(
                 lhs, rhs, (((1,), (1,)), ((), ())), preferred_element_type=jnp.float32)
 
-        def begin(self):
+        def product(self):
             j = self.j
-            if self.turned:
-                self.begin_turned()
-            elif j < 4:
-                for d in self.ds:
-                    rows_j = full[pl.ds(q(0), quarter), :] if j == 0 else chunk[j - 1]
-                    self.multiply(d, rows_j, full[pl.ds(q(DELTA[d]), quarter), :])
-            else:
+            if self.split:
                 @pl.when(low)
                 def _():
                     for d in self.ds:
@@ -172,21 +169,13 @@
                 def _():
                     for d in self.ds:
                         self.multiply(d, full[pl.ds(q(DELTA[d]), quarter), :], chunk[3, half:])
-            start(self.a, self.b)
-
-        def begin_turned(self):
-            if self.j == 0:
-                for d in self.ds:
-                    self.multiply(d, fully[:, y], fully[d])
-            else:
-                @pl.when(low)
-                def _():
-                    self.multiply(self.ds[0], chunky[1], fully[self.ds[0] // 2])
-
-                @pl.when(~low)
-                def _():
-                    for d in self.ds:
-                        self.multiply(d, fully[:, (y + d) % 4], chunky[1, 2:])
+                return
+            for d in self.ds:
+                if self.turned:
+                    self.multiply(d, fully[:, y] if j == 0 else chunky[1], fully[d])
+                else:
+                    rows_j = full[pl.ds(q(0), quarter), :] if j == 0 else chunk[j - 1]
+                    self.multiply(d, rows_j, full[pl.ds(q(DELTA[d]), quarter), :])
 
         def middle(self):
             j = self.j
@@ -208,7 +197,7 @@
             j = self.j
             arrived(self.c, self.d)
             total = part[j, self.strip(0), self.whole] + sum2[0, j, :, self.whole] + sum2[1, j, :, self.whole]
-            if j == 4:
+            if self.split:
                 @pl.when(low)
                 def _():
                     self.place(total)
@@ -217,7 +206,7 @@
                 def _():
                     mine[2, :, self.whole] = total
                     start(*self.sends)
-            elif j % 2:
+            elif self.sends:
                 mine[j // 2, :, self.whole] = total
                 start(*self.sends)
             else:
@@ -225,16 +214,16 @@
 
         def receive(self):
             arrived(*self.sends)
-            if self.j == 4:
-                for d in self.ds:
-                    first = pl.multiple_of(q(4 - DELTA[d]) + half, half)
-                    out_ref[4, :, pl.ds(first, half)] = theirs[2, :, pl.ds(d * half, half)]
-            else:
+            if not self.split:
                 self.place(theirs[self.j // 2, :, self.whole])
+                return
+            for d in self.ds:
+                first = pl.multiple_of(q(4 - DELTA[d]) + half, half)
+                out_ref[4, :, pl.ds(first, half)] = theirs[2, :, pl.ds(d * half, half)]
 
         def settle(self):
             left(self.a, self.b, self.c, self.d)
-            if self.j != 4:
+            if not self.split:
                 left(*self.sends)
 
     u00, u10 = Unit(0, 0, 1), Unit(1, 0, 1)
@@ -247,13 +236,14 @@
     v00, v01 = Unit(0, 0, 2, turned=True), Unit(0, 2, 2, turned=True)
     v40, v41 = Unit(4, 0, 2, turned=True), Unit(4, 2, 2, turned=True)
     always = (u10, u11, u20, u21, u12, u22, u13, u23, u30, u31)
-    even_only, odd_only = (u00, u01, u02, u03, u40, u41), (v00, v01, v40, v41)
-
-    def receive_turned():
-        arrived(*v40.sends, *v41.sends)
-        cols_of = [theirs[2, :, pl.ds(pl.multiple_of((y + 4 - i) % 4 * half, half), half)] for i in range(4)]
-        out_ref[4, :, pl.ds(2 * quarter, quarter)] = jnp.concatenate([v[:, :strip] for v in cols_of], axis=1)
-        out_ref[4, :, pl.ds(3 * quarter, quarter)] = jnp.concatenate([v[:, strip:] for v in cols_of], axis=1)
+    even_only, odd_only = (u00, u01, u02, u03, u40, u41), (v00, v01)
+
+    def begin(*units):
+        for i in range(0, len(units), 2):
+            for u in units[i:i + 2]:
+                u.product()
+            for u in units[i:i + 2]:
+                start(u.a, u.b)
 
     def both(*steps):
         for step in steps:
@@ -267,8 +257,11 @@
             start(m1[0], p1[0], m1[1], p1[1])
         own_piece(0, 0)
         own_piece(0, 1)
+        if not is_odd:
+            start(w1[0])
         if is_odd:
-            start(g1, h1, g2, h2, y1[0])
+            start(g1, h1, g2, h2)
+            pl.when(~low)(y1[0].start)
         arrived(m2)
         start(m3)
         arrived(p2)
@@ -289,6 +282,7 @@
             arrived(p1[h])
             own_piece(1, h)
         if not is_odd:
+            start(w1[3])
             start(*rest)
         arrived(m3)
         own_piece(2, 0)
@@ -297,70 +291,91 @@
 
     def even_core():
         head(False)
-        u00.begin()
+        begin(u00)
+        forward(w1, w2, shards=(0,))
         forward(x1, x2, shards=(3, 1, 2))
-        u10.begin()
+        begin(u10)
         arrived(m4, p7)
         start(p8)
         arrived(p9)
-        both(u01.begin, u11.begin, u00.middle, u10.middle)
-        forward(x2, x3, shards=(0, 3))
+        begin(u01, u11)
+        both(u00.middle, u10.middle)
+        forward(w1, w2, shards=(3,))
+        arrived(x2[0], x2[3])
         arrived(m9, m7)
         start(m8)
         arrived(p4)
         pl.semaphore_signal(gate, inc=1, device_id=gp, device_id_type=MESH)
-        both(u02.begin, u12.begin, u01.middle, u11.middle)
+        begin(u02, u12)
+        both(u01.middle, u11.middle)
         forward(x2, x3, shards=(1, 2))
-        both(u20.begin, u21.begin, u22.begin, u12.middle, u02.middle)
+        begin(u20, u21, u22)
+        both(u12.middle, u02.middle)
         arrived(m5, p5, m8, p8)
-        both(u03.begin, u13.begin, u23.begin, u20.middle, u21.middle, u22.middle)
+        begin(u03, u13, u23)
+        both(u20.middle, u21.middle, u22.middle)
         arrived(*x3)
-        both(u30.begin, u31.begin)
-        both(u13.middle, u03.middle, u10.end, u11.end, u00.end, u01.end, u30.middle, u31.middle, u12.end)
+        begin(u30, u31)
+        both(u13.middle, u03.middle, u10.end, u11.end, u00.end, u01.end)
         arrived(*x4)
-        both(u40.begin, u41.begin, u23.middle)
-        both(u13.end, u02.end, u20.end, u21.end, u22.end)
-        both(u40.middle, u41.middle)
-        both(u30.end, u31.end, u40.end, u41.end, u03.end, u23.end)
+        begin(u40, u41)
+        both(u30.middle, u31.middle, u12.end, u02.end)
+        both(u40.middle, u41.middle, u23.middle)
+        both(u13.end, u40.end, u41.end, u30.end, u31.end, u20.end, u21.end, u22.end, u03.end, u23.end)
+
+    def pass_on(*shards):
+        for r in shards:
+            arrived(w2[r] if r in w2 else x3[r])
+            x4[r].start()
 
     def odd_core():
         head(True)
+        pl.when(relays)(lambda: forward(y1, y2, shards=(0,)))
         forward(x1, x2, shards=(3, 1))
         arrived(g2)
-        start(y1[3])
+        pl.when(~low)(y1[3].start)
         arrived(h2)
-        start(y1[1])
+        pl.when(~low)(y1[1].start)
         pl.semaphore_wait(gate, 1)
         start(m4, p7, *rest)
         forward(x1, x2, shards=(2,))
-        u10.begin()
+        begin(u10)
         arrived(g3, h3)
-        start(y1[2])
+        pl.when(~low)(y1[2].start)
         forward(x2, x3, shards=(0, 3))
         u10.middle()
+        pl.when(relays)(lambda: forward(y1, y2, shards=(3,)))
         forward(x2, x3, shards=(1,))
         arrived(m4, p7)
         start(p8)
         arrived(p9)
-        u11.begin()
+        begin(u11)
         forward(x2, x3, shards=(2,))
-        both(u20.begin, u21.begin)
-        forward(y1, y2, shards=(0, 3, 1))
+        begin(u20, u21)
+        pl.when(relays)(lambda: forward(y1, y2, shards=(1, 2)))
         arrived(m9, m7)
         start(m8)
         arrived(p4)
-        both(u12.begin, u22.begin, u11.middle, u20.middle, u21.middle)
-        forward(y1, y2, shards=(2,))
+        begin(u12, u22)
+        both(u11.middle, u20.middle, u21.middle)
+        pass_on(0, 3, 1, 2)
         arrived(m5, p5, m8, p8)
-        both(u13.begin, u23.begin, v00.begin, v01.begin)
-        forward(x3, x4, shards=(0, 3))
+        begin(u13, u23, u30, u31)
         both(u12.middle)
-        forward(x3, x4, shards=(1, 2))
-        both(u30.begin, u31.begin, u13.middle, v00.middle, v01.middle)
-        arrived(*y2)
-        both(v40.begin, v41.begin, u10.end, u11.end, u20.end, u21.end, u12.end)
-        both(u30.middle, u31.middle, v40.middle, v41.middle, u22.middle, u23.middle)
-        both(v00.end, v01.end, v40.end, v41.end, u13.end, u30.end, u31.end, u22.end, u23.end)
+        begin(v00, v01)
+        both(u13.middle)
+
+        def last_pair():
+            arrived(*y2)
+            begin(v40, v41)
+
+        pl.when(low)(last_pair)
+        both(u10.end, u11.end, u20.end, u21.end, u12.end, v00.middle, v01.middle)
+        both(u30.middle, u31.middle)
+        both(u22.middle, u23.middle)
+        pl.when(low)(lambda: both(v40.middle, v41.middle))
+        both(u13.end, u30.end, u31.end, v00.end, v01.end, u22.end, u23.end)
+        pl.when(low)(lambda: both(v40.end, v41.end))
 
     pl.when(~odd)(even_core)
     pl.when(odd)(odd_core)
@@ -370,15 +385,11 @@
     def _():
         both(u40.receive, u41.receive)
 
-    @pl.when(low & odd)
-    def _():
-        receive_turned()
-
     @pl.when(~low)
     def _():
         out_ref[4] = jnp.zeros(out_ref.shape[1:], out_ref.dtype)
 
-    left(*m1, *p1, m2, p2, m3, p3, m4, p4, m5, p5, m7, p7, m8, p8, m9, p9, *x2, *x3)
+    left(*m1, *p1, m2, p2, m3, p3, m4, p4, m5, p5, m7, p7, m8, p8, m9, p9, *x2, x3[1], x3[2])
     for r in range(4):
         left(*x1[r])
     for u in always:
@@ -386,22 +397,26 @@
 
     @pl.when(odd)
     def _():
-        left(*x4, *y1, *y2, g1, h1, g2, h2, g3, h3)
+        left(g1, h1, g2, h2, g3, h3, x3[0], x3[3], *x4)
         for u in odd_only:
             u.settle()
 
     @pl.when(~odd)
     def _():
+        left(w1[0], w1[3], w2[0], w2[3])
         for u in even_only:
             u.settle()
 
-    @pl.when(~low & odd)
-    def _():
-        left(*v40.sends, *v41.sends)
+    @pl.when(low & odd)
+    def _():
+        both(v40.settle, v41.settle)
 
     @pl.when(~low & ~odd)
     def _():
         left(*u40.sends, *u41.sends)
+
+    pl.when(odd & ~low)(lambda: left(*y1))
+    pl.when(relays)(lambda: left(*y2))
 
 def solution(mesh):
     def local_fn(a_blk):
@@ -417,6 +432,7 @@
                 pltpu.VMEM((4, 4, strip, 4 * cols), jnp.bfloat16),
                 pltpu.VMEM((4, rows // 4, 4 * cols), jnp.bfloat16),
                 pltpu.VMEM((2, 4, strip, 4 * cols), jnp.bfloat16),
+                pltpu.VMEM((rows // 4, 2 * cols), jnp.bfloat16),
                 pltpu.VMEM((5, rows // 4, rows), jnp.float32),
                 pltpu.VMEM((2, 5, strip, rows // 2), jnp.float32),
                 pltpu.VMEM((2, 5, strip, rows), jnp.float32),

time: 70 us -> 68.4 us (0.977); the launches traced: 68.8 us -> 68.3 us
  no operation moved by 1% of the time
where the time goes in v4:
time: 68.4 us; the launch traced here: 68.3 us
  Pallas kernels  67.2 us (98%)
  local copies, waits for them, and re-layouts  1.06 us (2%)
    pallas_call x1, Pallas kernels, local_fn(): pl.pallas_call(kernel, out_shape=jax.ShapeDtypeStruct((5, strip, rows), j...  67.2 us

profile of v4, /device:TPU:1, one launch (start us, length us, event | category | flops | bytes accessed | tf_op | source)
XLA Modules:
  0.0 68.3 jit_solution(10570165818867910243)
XLA Ops:
  0.0 67.2 %shard_map.17 = f32[5,64,1024]{2,1,0:T(8,128)S(1)} custom-call(bf16[1024,512]{1,0:T(8,128)(2,1)} %a_hbm.1, bf16[4,4,64,512]{3,2,1,0:T(8,128)(2,1)} %bitcast.3), custom_call_target="tpu_custom_call" | custom-call | tf_op jit(solution)/shard_map/pallas_call | solution.py:425
  67.2 1.1 %copy.3 = f32[1,5,64,1024]{3,2,1,0:T(8,128)} copy(f32[1,5,64,1024]{3,2,1,0:T(8,128)S(1)} %bitcast.2) | data formatting | bytes 2621440

commit v5 on v4

--- a/solution.py
+++ b/solution.py
@@ -299,13 +299,14 @@
         start(p8)
         arrived(p9)
         begin(u01, u11)
-        both(u00.middle, u10.middle)
-        forward(w1, w2, shards=(3,))
-        arrived(x2[0], x2[3])
+        u00.middle()
         arrived(m9, m7)
         start(m8)
         arrived(p4)
         pl.semaphore_signal(gate, inc=1, device_id=gp, device_id_type=MESH)
+        u10.middle()
+        forward(w1, w2, shards=(3,))
+        arrived(x2[0], x2[3])
         begin(u02, u12)
         both(u01.middle, u11.middle)
         forward(x2, x3, shards=(1, 2))
@@ -316,12 +317,12 @@
         both(u20.middle, u21.middle, u22.middle)
         arrived(*x3)
         begin(u30, u31)
-        both(u13.middle, u03.middle, u10.end, u11.end, u00.end, u01.end)
+        both(u13.middle, u10.end, u11.end, u00.end, u01.end)
         arrived(*x4)
         begin(u40, u41)
         both(u30.middle, u31.middle, u12.end, u02.end)
-        both(u40.middle, u41.middle, u23.middle)
-        both(u13.end, u40.end, u41.end, u30.end, u31.end, u20.end, u21.end, u22.end, u03.end, u23.end)
+        both(u40.middle, u41.middle, u03.middle, u23.middle)
+        both(u13.end, u20.end, u21.end, u22.end, u30.end, u31.end, u40.end, u41.end, u03.end, u23.end)
 
     def pass_on(*shards):
         for r in shards:
@@ -344,21 +345,22 @@
         pl.when(~low)(y1[2].start)
         forward(x2, x3, shards=(0, 3))
         u10.middle()
-        pl.when(relays)(lambda: forward(y1, y2, shards=(3,)))
         forward(x2, x3, shards=(1,))
         arrived(m4, p7)
         start(p8)
         arrived(p9)
         begin(u11)
+        pl.when(relays)(lambda: forward(y1, y2, shards=(3,)))
         forward(x2, x3, shards=(2,))
         begin(u20, u21)
-        pl.when(relays)(lambda: forward(y1, y2, shards=(1, 2)))
+        pass_on(0, 3)
         arrived(m9, m7)
         start(m8)
         arrived(p4)
         begin(u12, u22)
         both(u11.middle, u20.middle, u21.middle)
-        pass_on(0, 3, 1, 2)
+        pass_on(1, 2)
+        pl.when(relays)(lambda: forward(y1, y2, shards=(1, 2)))
         arrived(m5, p5, m8, p8)
         begin(u13, u23, u30, u31)
         both(u12.middle)

time: 68.4 us -> 67.2 us (0.982)
  Pallas kernels: 67.2 us -> 66 us
    pallas_call x1, Pallas kernels: 67.2 us -> 66 us  [local_fn(): pl.pallas_call(kernel, out_shape=jax.ShapeDtypeStruct((5, strip, rows), j...]
where the time goes in v5:
time: 67.2 us; the launch traced here: 67.1 us
  Pallas kernels  66 us (98%)
  local copies, waits for them, and re-layouts  1.06 us (2%)
    pallas_call x1, Pallas kernels, local_fn(): pl.pallas_call(kernel, out_shape=jax.ShapeDtypeStruct((5, strip, rows), j...  66 us

profile of v5, /device:TPU:1, one launch (start us, length us, event | category | flops | bytes accessed | tf_op | source)
XLA Modules:
  0.0 67.1 jit_solution(8004306660568282258)
XLA Ops:
  0.0 66.0 %shard_map.17 = f32[5,64,1024]{2,1,0:T(8,128)S(1)} custom-call(bf16[1024,512]{1,0:T(8,128)(2,1)} %a_hbm.1, bf16[4,4,64,512]{3,2,1,0:T(8,128)(2,1)} %bitcast.3), custom_call_target="tpu_custom_call" | custom-call | tf_op jit(solution)/shard_map/pallas_call | solution.py:427
  66.0 1.1 %copy.3 = f32[1,5,64,1024]{3,2,1,0:T(8,128)} copy(f32[1,5,64,1024]{3,2,1,0:T(8,128)S(1)} %bitcast.2) | data formatting | bytes 2621440

commit v6 on v5

--- a/solution.py
+++ b/solution.py
@@ -320,9 +320,9 @@
         both(u13.middle, u10.end, u11.end, u00.end, u01.end)
         arrived(*x4)
         begin(u40, u41)
-        both(u30.middle, u31.middle, u12.end, u02.end)
-        both(u40.middle, u41.middle, u03.middle, u23.middle)
-        both(u13.end, u20.end, u21.end, u22.end, u30.end, u31.end, u40.end, u41.end, u03.end, u23.end)
+        both(u30.middle, u12.end, u02.end)
+        both(u40.middle, u41.middle, u31.middle, u03.middle, u23.middle)
+        both(u13.end, u20.end, u21.end, u22.end, u30.end, u40.end, u41.end, u31.end, u03.end, u23.end)
 
     def pass_on(*shards):
         for r in shards:
@@ -358,22 +358,23 @@
         start(m8)
         arrived(p4)
         begin(u12, u22)
+        pl.when(relays)(lambda: forward(y1, y2, shards=(1,)))
         both(u11.middle, u20.middle, u21.middle)
         pass_on(1, 2)
-        pl.when(relays)(lambda: forward(y1, y2, shards=(1, 2)))
+        pl.when(relays)(lambda: forward(y1, y2, shards=(2,)))
         arrived(m5, p5, m8, p8)
         begin(u13, u23, u30, u31)
         both(u12.middle)
         begin(v00, v01)
-        both(u13.middle)
 
         def last_pair():
             arrived(*y2)
             begin(v40, v41)
 
         pl.when(low)(last_pair)
-        both(u10.end, u11.end, u20.end, u21.end, u12.end, v00.middle, v01.middle)
-        both(u30.middle, u31.middle)
+        both(u13.middle)
+        both(u10.end, u11.end, u20.end, u21.end, v00.middle, v01.middle)
+        both(u30.middle, u31.middle, u12.end)
         both(u22.middle, u23.middle)
         pl.when(low)(lambda: both(v40.middle, v41.middle))
         both(u13.end, u30.end, u31.end, v00.end, v01.end, u22.end, u23.end)

time: 67.2 us -> 66.8 us (level)
  no operation moved by 1% of the time
where the time goes in v6:
time: 66.8 us; the launch traced here: 66.7 us
  Pallas kernels  65.6 us (98%)
  local copies, waits for them, and re-layouts  1.06 us (2%)
    pallas_call x1, Pallas kernels, local_fn(): pl.pallas_call(kernel, out_shape=jax.ShapeDtypeStruct((5, strip, rows), j...  65.6 us

profile of v6, /device:TPU:1, one launch (start us, length us, event | category | flops | bytes accessed | tf_op | source)
XLA Modules:
  0.0 66.7 jit_solution(16091028978579944646)
XLA Ops:
  0.0 65.6 %shard_map.17 = f32[5,64,1024]{2,1,0:T(8,128)S(1)} custom-call(bf16[1024,512]{1,0:T(8,128)(2,1)} %a_hbm.1, bf16[4,4,64,512]{3,2,1,0:T(8,128)(2,1)} %bitcast.3), custom_call_target="tpu_custom_call" | custom-call | tf_op jit(solution)/shard_map/pallas_call | solution.py:428
  65.6 1.1 %copy.3 = f32[1,5,64,1024]{3,2,1,0:T(8,128)} copy(f32[1,5,64,1024]{3,2,1,0:T(8,128)S(1)} %bitcast.2) | data formatting | bytes 2621440

commit v7 on v6

--- a/solution.py
+++ b/solution.py
@@ -337,12 +337,12 @@
         pl.when(~low)(y1[3].start)
         arrived(h2)
         pl.when(~low)(y1[1].start)
+        arrived(g3, h3)
+        pl.when(~low)(y1[2].start)
         pl.semaphore_wait(gate, 1)
         start(m4, p7, *rest)
         forward(x1, x2, shards=(2,))
         begin(u10)
-        arrived(g3, h3)
-        pl.when(~low)(y1[2].start)
         forward(x2, x3, shards=(0, 3))
         u10.middle()
         forward(x2, x3, shards=(1,))

time: 66.8 us -> 66.8 us (level)
  no operation moved by 1% of the time
where the time goes in v7:
time: 66.8 us; the launch traced here: 66.7 us
  Pallas kernels  65.6 us (98%)
  local copies, waits for them, and re-layouts  1.06 us (2%)
    pallas_call x1, Pallas kernels, local_fn(): pl.pallas_call(kernel, out_shape=jax.ShapeDtypeStruct((5, strip, rows), j...  65.6 us

profile of v7, /device:TPU:1, one launch (start us, length us, event | category | flops | bytes accessed | tf_op | source)
XLA Modules:
  0.0 66.7 jit_solution(2287261150214995360)
XLA Ops:
  0.0 65.6 %shard_map.17 = f32[5,64,1024]{2,1,0:T(8,128)S(1)} custom-call(bf16[1024,512]{1,0:T(8,128)(2,1)} %a_hbm.1, bf16[4,4,64,512]{3,2,1,0:T(8,128)(2,1)} %bitcast.3), custom_call_target="tpu_custom_call" | custom-call | tf_op jit(solution)/shard_map/pallas_call | solution.py:428
  65.6 1.1 %copy.3 = f32[1,5,64,1024]{3,2,1,0:T(8,128)} copy(f32[1,5,64,1024]{3,2,1,0:T(8,128)S(1)} %bitcast.2) | data formatting | bytes 2621440
